TPU v7x, 8 devices: a whole 2x2x1 slice. The times are simulated.
8 devices in a mesh: dp: 2 (over z, y), cp: 4 (over x, core).
Axes of the slice: x: 2, y: 2, z: 1, core: 2. Of those that a mesh axis runs over, the one named last changes fastest.
Arguments:
- hidden: bfloat16 [24, 1536, 2048], P('dp', 'cp')
- positions: int32 [1536], P('cp')
- w_q: bfloat16 [2048, 2048], replicated
- w_k: bfloat16 [2048, 2048], replicated
- w_v: bfloat16 [2048, 2048], replicated
- w_o: bfloat16 [2048, 2048], replicated
Outputs:
- output 1: bfloat16 [24, 1536, 2048], P('dp', 'cp')
- output 2: float32 [16], replicated
- output 3: bfloat16 [2048, 2048], replicated
- output 4: bfloat16 [2048, 2048], replicated
All inputs are finite; a program needn't handle non-finite values.
Results may differ from a plain program's by a relative error of at most 0.00772671.
Values are sent between devices in bfloat16 or wider.
A program may use at most 1 GiB of HBM per device.

v0:
```python
import jax
import jax.numpy as jnp
from jax import lax
from jax.sharding import PartitionSpec as P

HEAD_DIM = 128
TAU_CLIP = 100.0
ROPE_THETA = 50000.0


def rope_tables(pos_ids):
    half_dim = HEAD_DIM // 2
    inv_freq = jnp.float32(ROPE_THETA) ** (-jnp.arange(half_dim, dtype=jnp.float32) * (2.0 / HEAD_DIM))
    angle = pos_ids.astype(jnp.float32)[:, None] * inv_freq[None, :]
    return jnp.cos(angle)[None, :, None, :], jnp.sin(angle)[None, :, None, :]


def rope_rotate(tensor, cos_t, sin_t):
    half_dim = HEAD_DIM // 2
    lead_half = tensor[..., :half_dim]
    tail_half = tensor[..., half_dim:]
    return jnp.concatenate([lead_half * cos_t - tail_half * sin_t, tail_half * cos_t + lead_half * sin_t], axis=-1)


def project_heads(hidden, pos_ids, w_q, w_k, w_v):
    batch_n, seq_n, _ = hidden.shape
    head_shape = (batch_n, seq_n, w_q.shape[1] // HEAD_DIM, HEAD_DIM)
    cos_t, sin_t = rope_tables(pos_ids)
    q_heads = rope_rotate(jnp.dot(hidden, w_q, preferred_element_type=jnp.float32).reshape(head_shape), cos_t, sin_t).astype(jnp.bfloat16)
    k_heads = rope_rotate(jnp.dot(hidden, w_k, preferred_element_type=jnp.float32).reshape(head_shape), cos_t, sin_t).astype(jnp.bfloat16)
    v_heads = jnp.dot(hidden, w_v, preferred_element_type=jnp.float32).astype(jnp.bfloat16).reshape(head_shape)
    return q_heads, k_heads, v_heads


def empty_state(batch_n, seq_n, n_heads):
    row_shape = (batch_n, n_heads, seq_n)
    return (jnp.full(row_shape, -jnp.inf, jnp.float32), jnp.zeros(row_shape, jnp.float32),
            jnp.zeros((batch_n, seq_n, n_heads, HEAD_DIM), jnp.float32), jnp.full((n_heads,), -jnp.inf, jnp.float32))


def attend_block(q_heads, k_blk, v_blk, state, allowed):
    run_max, run_sum, out_acc, head_max = state
    scores = jnp.einsum("bqhd,bkhd->bhqk", q_heads, k_blk, preferred_element_type=jnp.float32) * (HEAD_DIM ** -0.5)
    if allowed is not None:
        scores = jnp.where(allowed, scores, -jnp.inf)
    head_max = jnp.maximum(head_max, jnp.max(scores, axis=(0, 2, 3)))
    new_max = jnp.maximum(run_max, jnp.max(scores, axis=-1))
    rescale = jnp.exp(run_max - new_max)
    prob_w = jnp.exp(scores - new_max[..., None])
    new_sum = run_sum * rescale + jnp.sum(prob_w, axis=-1)
    part_pv = jnp.einsum("bhqk,bkhd->bqhd", prob_w.astype(jnp.bfloat16), v_blk, preferred_element_type=jnp.float32)
    new_acc = out_acc * jnp.transpose(rescale, (0, 2, 1))[..., None] + part_pv
    return new_max, new_sum, new_acc, head_max


def finish_attn(state, w_o):
    run_max, run_sum, out_acc, head_max = state
    batch_n, seq_n, n_heads, _ = out_acc.shape
    attn_val = (out_acc / jnp.transpose(run_sum, (0, 2, 1))[..., None]).astype(jnp.bfloat16)
    attn_val = attn_val.reshape(batch_n, seq_n, n_heads * HEAD_DIM)
    return jnp.dot(attn_val, w_o, preferred_element_type=jnp.float32).astype(jnp.bfloat16), head_max


def clip_weights(head_max, w_q, w_k):
    factor = jnp.where(head_max > TAU_CLIP, jnp.sqrt(TAU_CLIP / head_max), 1.0)
    col_factor = jnp.repeat(factor, HEAD_DIM)[None, :]
    return (w_q.astype(jnp.float32) * col_factor).astype(jnp.bfloat16), (w_k.astype(jnp.float32) * col_factor).astype(jnp.bfloat16)


def solution(mesh):
    cp_size = mesh.shape["cp"]
    shift_pairs = [(src_rank, (src_rank + 1) % cp_size) for src_rank in range(cp_size)]

    def device_body(hidden, pos_ids, w_q, w_k, w_v, w_o):
        cp_rank = lax.axis_index("cp")
        q_heads, k_heads, v_heads = project_heads(hidden, pos_ids, w_q, w_k, w_v)
        batch_n, seq_n, n_heads, _ = q_heads.shape
        causal = lax.broadcasted_iota(jnp.int32, (seq_n, seq_n), 0) >= lax.broadcasted_iota(jnp.int32, (seq_n, seq_n), 1)
        state = attend_block(q_heads, k_heads, v_heads, empty_state(batch_n, seq_n, n_heads), causal)

        def step(step_idx, carried):
            k_blk, v_blk, attn_state = carried
            k_blk = lax.ppermute(k_blk, "cp", shift_pairs)
            v_blk = lax.ppermute(v_blk, "cp", shift_pairs)

            def use_block(state_in):
                return attend_block(q_heads, k_blk, v_blk, state_in, None)

            def skip_block(state_in):
                return state_in

            attn_state = lax.cond(step_idx <= cp_rank, use_block, skip_block, attn_state)
            return k_blk, v_blk, attn_state

        _, _, state = lax.fori_loop(1, cp_size, step, (k_heads, v_heads, state))
        attn_out, head_max = finish_attn(state, w_o)
        head_max = lax.pmax(head_max, ("dp", "cp"))
        w_q_new, w_k_new = clip_weights(head_max, w_q, w_k)
        return attn_out, head_max, w_q_new, w_k_new

    return jax.shard_map(
        device_body,
        mesh=mesh,
        in_specs=(P("dp", "cp", None), P("cp"), P(None, None), P(None, None), P(None, None), P(None, None)),
        out_specs=(P("dp", "cp", None), P(None), P(None, None), P(None, None)),
        check_vma=False,
    )
```

profile of v0, /device:TPU:0, one launch (start us, length us, event | category | flops | bytes accessed | tf_op | source)
XLA Modules:
  0.0 2594.3 jit_solution(2517963470601334881)
XLA Ops:
  0.6 47.0 %fusion.23 = f32[12,384,2048]{2,1,0:T(8,128)} fusion(bf16[12,384,2048]{2,1,0:T(8,128)(2,1)} %param.10, bf16[2048,2048]{1,0:T(8,128)(2,1)} %param.12), kind=kOutput, calls=%fused_computation.38 | convolution fusion | flops 38654705664 | bytes 65011712 | tf_op jit(solution)/shard_map/dot_general | solution.py:29
  47.7 32.7 %copy.39 = f32[576,8,16,128]{3,2,1,0:T(8,128)} copy(f32[576,8,16,128]{3,1,2,0:T(8,128)} %bitcast.53) | data formatting | bytes 75497472
  80.4 51.7 %fusion.32 = (f32[12,384,16,64]{3,2,1,0:T(8,128)}, f32[12,384,16,64]{3,2,1,0:T(8,128)}) fusion(f32[12,384,16,128]{3,2,1,0:T(8,128)} %bitcast.51), kind=kLoop, calls=%fused_computation.54 | loop fusion | bytes 75497472 | tf_op jit(solution)/shard_map/slice | solution.py:20
  132.1 45.2 %fusion.26 = f32[12,384,2048]{2,1,0:T(8,128)} fusion(bf16[12,384,2048]{2,1,0:T(8,128)(2,1)} %param.10, bf16[2048,2048]{1,0:T(8,128)(2,1)S(1)} %bitcast.59), kind=kOutput, calls=%fused_computation.41 | convolution fusion | flops 38654705664 | bytes 65011712 | tf_op jit(solution)/shard_map/dot_general | solution.py:30
  210.0 51.3 %fusion.33 = (f32[12,384,16,64]{3,2,1,0:T(8,128)}, f32[12,384,16,64]{3,2,1,0:T(8,128)}) fusion(f32[12,384,16,128]{3,2,1,0:T(8,128)} %bitcast.52), kind=kLoop, calls=%fused_computation.55 | loop fusion | bytes 75497472 | tf_op jit(solution)/shard_map/slice | solution.py:20
  262.1 107.3 %subtract_convert_fusion = (bf16[12,384,16,64]{3,1,2,0:T(8,128)(2,1)}, bf16[12,384,16,64]{3,1,2,0:T(8,128)(2,1)}, bf16[12,384,16,64]{3,1,2,0:T(8,128)(2,1)}, bf16[12,384,16,64]{3,1,2,0:T(8,128)(2,1)}) fusion(f32[12,384,16,64]{3,2,1,0:T(8,128)} %get-tuple-element.253, f32[12,384,16,64]{3,2,1,0:T(8,128)} %get-tuple-element.252, ...), kind=kLoop, calls=%fused_computation.27 | loop fusion | flops 75497472 | bytes 113442816 | tf_op jit(solution)/shard_map/convert
  369.4 43.4 %pad_maximum_fusion = (bf16[12,384,16,128]{3,1,2,0:T(8,128)(2,1)}, bf16[12,384,16,128]{3,1,2,0:T(8,128)(2,1)}) fusion(bf16[12,384,16,64]{3,1,2,0:T(8,128)(2,1)} %get-tuple-element.256, bf16[12,384,16,64]{3,1,2,0:T(8,128)(2,1)} %get-tuple-element.257, bf16[12,384,16,64]{3,1,2,0:T(8,128)(2,1)} %get-tuple-element.249, ...), kind=kLoop, calls=%fused_computation.31 | loop fusion | flops 75497472 | bytes 75497472 | tf_op jit(solution)/shard_map/concatenate | solution.py:22
  412.9 50.9 %fusion.13 = (f32[12,16,384]{2,1,0:T(8,128)S(1)}, f32[12,16,384,384]{2,3,1,0:T(8,128)}) fusion(pred[384,384]{0,1:T(8,128)(4,1)S(1)} %iota_compare_fusion, bf16[12,384,16,128]{3,1,2,0:T(8,128)(2,1)} %get-tuple-element.347, bf16[12,384,16,128]{3,1,2,0:T(8,128)(2,1)} %get-tuple-element.340), kind=kOutput, calls=%fused_computation.18 | convolution fusion | flops 7332618240 | bytes 151437312 | tf_op jit(solution)/shard_map/bqhd,bkhd->bhqk/dot_general | solution.py:43
  463.7 38.4 %fusion.12 = (f32[16]{0:T(128)}, f32[12,16,384]{2,1,0:T(8,128)S(1)}) fusion(f32[12,16,384,384]{2,3,1,0:T(8,128)} %get-tuple-element.265, pred[384,384]{0,1:T(8,128)(4,1)S(1)} %iota_compare_fusion, f32[12,16,384]{2,1,0:T(8,128)S(1)} %get-tuple-element.342), kind=kLoop, calls=%fused_computation.17 | loop fusion | flops 141484016 | bytes 113983552 | tf_op jit(solution)/shard_map/reduce_max | solution.py:46
  502.9 46.0 %convert_bitcast_fusion = bf16[12,48,16,8,128]{4,3,2,1,0:T(8,128)(2,1)} fusion(bf16[12,384,2048]{2,1,0:T(8,128)(2,1)} %param.10, bf16[2048,2048]{1,0:T(8,128)(2,1)} %param.14), kind=kOutput, calls=%fused_computation.33 | convolution fusion | flops 38664142848 | bytes 46137344 | tf_op jit(solution)/shard_map/dot_general | solution.py:31
  548.9 56.4 %bitcast_add_fusion.1 = f32[12,384,16,128]{1,3,2,0:T(8,128)} fusion(f32[12,384,16]{1,2,0:T(8,128)S(1)} %get-tuple-element.258, f32[12,16,384,384]{2,3,1,0:T(8,128)} %get-tuple-element.265, f32[12,16,384]{2,1,0:T(8,128)S(1)} %get-tuple-element.342, pred[384,384]{0,1:T(8,128)(4,1)S(1)} %iota_compare_fusion, bf16[12,48,16,8,128]{4,3,2,1,0:T(8,128)(2,1)} %convert_bitcast_fusion), kind=kOutput, calls=%fused_computation.24 | convolution fusion | flops 7370440704 | bytes 170606592 | tf_op jit(solution)/shard_map/bhqk,bkhd->bqhd/dot_general | solution.py:51
  605.3 36.7 %copy.27 = f32[12,384,16,128]{3,1,2,0:T(8,128)} copy(f32[12,384,16,128]{1,3,2,0:T(8,128)} %bitcast_add_fusion.1) | data formatting | bytes 75497472 | tf_op jit(solution)/shard_map/while | solution.py:95
  660.4 1647.0 %while.23 = (s32[]{:T(128)}, bf16[12,384,16,128]{3,1,2,0:T(8,128)(2,1)}, bf16[12,384,16,128]{3,1,2,0:T(8,128)(2,1)}, f32[12,16,384]{2,1,0:T(8,128)S(1)}, f32[12,...) while((s32[]{:T(128)}, ...), condition=%wide.region_9.10_spmd, body=%wide.region_3.9_spmd.sunk | while | flops 14769414144 | bytes 703070784 | solution.py:95
  663.9 202.8 %collective-permute-done = bf16[12,384,16,128]{3,1,2,0:T(8,128)(2,1)} collective-permute-done((bf16[12,384,16,128]{3,1,2,0:T(8,128)(2,1)}, bf16[12,384,16,128]{3,1,2,0:T(8,128)(2,1)}, u32[]{:S(2)}, u32[]{:S(2)}) %collective-permute-start) | collective-permute-done | bytes 18874400 | tf_op jit(solution)/shard_map/while/body/eval_jaxpr/ppermute | solution.py:83
  866.7 202.2 %collective-permute-done.1 = bf16[12,384,16,128]{3,1,2,0:T(8,128)(2,1)} collective-permute-done((bf16[12,384,16,128]{3,1,2,0:T(8,128)(2,1)}, bf16[12,384,16,128]{3,1,2,0:T(8,128)(2,1)}, u32[]{:S(2)}, u32[]{:S(2)}) %collective-permute-start.1) | collective-permute-done | bytes 18874400 | tf_op jit(solution)/shard_map/while/body/eval_jaxpr/ppermute | solution.py:84
  1106.5 157.9 %collective-permute-start = (bf16[12,384,16,128]{3,1,2,0:T(8,128)(2,1)}, bf16[12,384,16,128]{3,1,2,0:T(8,128)(2,1)}, u32[]{:S(2)}, u32[]{:S(2)}) collective-permute-start(bf16[12,384,16,128]{3,1,2,0:T(8,128)(2,1)} %get-tuple-element.350), channel_id=1, source_target_pairs={{0,1},{1,2},{2,3},{3,0},{4,5},{5,6},{6,7},{7,4}} | collective-permute-start | bytes 56623112 | tf_op jit(solution)/shard_map/while/body/eval_jaxpr/ppermute | solution.py:83
  1266.9 200.3 %collective-permute-done = bf16[12,384,16,128]{3,1,2,0:T(8,128)(2,1)} collective-permute-done((bf16[12,384,16,128]{3,1,2,0:T(8,128)(2,1)}, bf16[12,384,16,128]{3,1,2,0:T(8,128)(2,1)}, u32[]{:S(2)}, u32[]{:S(2)}) %collective-permute-start) | collective-permute-done | bytes 18874400 | tf_op jit(solution)/shard_map/while/body/eval_jaxpr/ppermute | solution.py:83
  1467.2 202.2 %collective-permute-done.1 = bf16[12,384,16,128]{3,1,2,0:T(8,128)(2,1)} collective-permute-done((bf16[12,384,16,128]{3,1,2,0:T(8,128)(2,1)}, bf16[12,384,16,128]{3,1,2,0:T(8,128)(2,1)}, u32[]{:S(2)}, u32[]{:S(2)}) %collective-permute-start.1) | collective-permute-done | bytes 18874400 | tf_op jit(solution)/shard_map/while/body/eval_jaxpr/ppermute | solution.py:84
  1709.4 160.5 %collective-permute-start.1 = (bf16[12,384,16,128]{3,1,2,0:T(8,128)(2,1)}, bf16[12,384,16,128]{3,1,2,0:T(8,128)(2,1)}, u32[]{:S(2)}, u32[]{:S(2)}) collective-permute-start(bf16[12,384,16,128]{3,1,2,0:T(8,128)(2,1)} %get-tuple-element.351), channel_id=1, source_target_pairs={{0,1},{1,2},{2,3},{3,0},{4,5},{5,6},{6,7},{7,4}} | collective-permute-start | bytes 56623112 | tf_op jit(solution)/shard_map/while/body/eval_jaxpr/ppermute | solution.py:84
  1869.8 197.8 %collective-permute-done = bf16[12,384,16,128]{3,1,2,0:T(8,128)(2,1)} collective-permute-done((bf16[12,384,16,128]{3,1,2,0:T(8,128)(2,1)}, bf16[12,384,16,128]{3,1,2,0:T(8,128)(2,1)}, u32[]{:S(2)}, u32[]{:S(2)}) %collective-permute-start) | collective-permute-done | bytes 18874400 | tf_op jit(solution)/shard_map/while/body/eval_jaxpr/ppermute | solution.py:83
  2067.6 202.2 %collective-permute-done.1 = bf16[12,384,16,128]{3,1,2,0:T(8,128)(2,1)} collective-permute-done((bf16[12,384,16,128]{3,1,2,0:T(8,128)(2,1)}, bf16[12,384,16,128]{3,1,2,0:T(8,128)(2,1)}, u32[]{:S(2)}, u32[]{:S(2)}) %collective-permute-start.1) | collective-permute-done | bytes 18874400 | tf_op jit(solution)/shard_map/while/body/eval_jaxpr/ppermute | solution.py:84
  2307.4 36.8 %copy.28 = f32[12,384,16,128]{1,3,2,0:T(8,128)} copy(f32[12,384,16,128]{3,1,2,0:T(8,128)} %get-tuple-element.201) | data formatting | bytes 75497472 | tf_op jit(solution)/shard_map/while | solution.py:95
  2359.1 44.0 %convolution_convert_fusion = bf16[12,384,2048]{2,1,0:T(8,128)(2,1)} fusion(bf16[12,384,2048]{1,2,0:T(8,128)(2,1)S(1)} %bitcast.55, bf16[2048,2048]{1,0:T(8,128)(2,1)} %param.15), kind=kOutput, calls=%fused_computation.36 | convolution fusion | flops 38664142848 | bytes 46137344 | tf_op jit(solution)/shard_map/dot_general | solution.py:61
  2403.2 178.1 %pmax.7 = f32[16]{0:T(128)S(1)} all-reduce(f32[16]{0:T(128)S(1)} %get-tuple-element.203), channel_id=1, replica_groups=mesh['dp'=2,'cp'=4] {'dp','cp'}, use_global_device_ids=true, to_apply=%region_10.11 | all-reduce | flops 16 | bytes 128 | tf_op jit(solution)/shard_map/pmax | solution.py:97
  (37 shorter events, 201.1 us)
Async XLA Ops:
  47.7 84.4 %slice-start = ((s8[8388608]{0:T(1024)(128)(4,1)}), s8[4194304]{0:T(1024)(128)(4,1)S(1)}, s32[]{:S(2)}) async-start(s8[8388608]{0:T(1024)(128)(4,1)} %bitcast.58), calls=%async_computation | async-start | bytes 8388608
  80.4 51.7 %slice-start.1 = ((s8[8388608]{0:T(1024)(128)(4,1)}), s8[4194304]{0:T(1024)(128)(4,1)S(1)}, s32[]{:S(2)}) async-start(s8[8388608]{0:T(1024)(128)(4,1)} %bitcast.58), calls=%async_computation.1 | async-start | bytes 8388608
  210.0 51.3 %copy-start.1 = (s32[384]{0:T(512)S(1)}, s32[384]{0:T(512)}, u32[]{:S(2)}) copy-start(s32[384]{0:T(512)} %param.11) | copy-start | bytes 4612
  642.0 18.4 copy-start
  642.0 18.4 copy-start.2
  660.4 206.3 %collective-permute-start = (bf16[12,384,16,128]{3,1,2,0:T(8,128)(2,1)}, bf16[12,384,16,128]{3,1,2,0:T(8,128)(2,1)}, u32[]{:S(2)}, u32[]{:S(2)}) collective-permute-start(bf16[12,384,16,128]{3,1,2,0:T(8,128)(2,1)} %get-tuple-element.350), channel_id=1, source_target_pairs={{0,1},{1,2},{2,3},{3,0},{4,5},{5,6},{6,7},{7,4}} | collective-permute-start | bytes 56623112 | tf_op jit(solution)/shard_map/while/body/eval_jaxpr/ppermute | solution.py:83
  661.3 407.7 %collective-permute-start.1 = (bf16[12,384,16,128]{3,1,2,0:T(8,128)(2,1)}, bf16[12,384,16,128]{3,1,2,0:T(8,128)(2,1)}, u32[]{:S(2)}, u32[]{:S(2)}) collective-permute-start(bf16[12,384,16,128]{3,1,2,0:T(8,128)(2,1)} %get-tuple-element.351), channel_id=1, source_target_pairs={{0,1},{1,2},{2,3},{3,0},{4,5},{5,6},{6,7},{7,4}} | collective-permute-start | bytes 56623112 | tf_op jit(solution)/shard_map/while/body/eval_jaxpr/ppermute | solution.py:84
  1106.5 360.7 %collective-permute-start = (bf16[12,384,16,128]{3,1,2,0:T(8,128)(2,1)}, bf16[12,384,16,128]{3,1,2,0:T(8,128)(2,1)}, u32[]{:S(2)}, u32[]{:S(2)}) collective-permute-start(bf16[12,384,16,128]{3,1,2,0:T(8,128)(2,1)} %get-tuple-element.350), channel_id=1, source_target_pairs={{0,1},{1,2},{2,3},{3,0},{4,5},{5,6},{6,7},{7,4}} | collective-permute-start | bytes 56623112 | tf_op jit(solution)/shard_map/while/body/eval_jaxpr/ppermute | solution.py:83
  1264.4 405.0 %collective-permute-start.1 = (bf16[12,384,16,128]{3,1,2,0:T(8,128)(2,1)}, bf16[12,384,16,128]{3,1,2,0:T(8,128)(2,1)}, u32[]{:S(2)}, u32[]{:S(2)}) collective-permute-start(bf16[12,384,16,128]{3,1,2,0:T(8,128)(2,1)} %get-tuple-element.351), channel_id=1, source_target_pairs={{0,1},{1,2},{2,3},{3,0},{4,5},{5,6},{6,7},{7,4}} | collective-permute-start | bytes 56623112 | tf_op jit(solution)/shard_map/while/body/eval_jaxpr/ppermute | solution.py:84
  1706.9 360.7 %collective-permute-start = (bf16[12,384,16,128]{3,1,2,0:T(8,128)(2,1)}, bf16[12,384,16,128]{3,1,2,0:T(8,128)(2,1)}, u32[]{:S(2)}, u32[]{:S(2)}) collective-permute-start(bf16[12,384,16,128]{3,1,2,0:T(8,128)(2,1)} %get-tuple-element.350), channel_id=1, source_target_pairs={{0,1},{1,2},{2,3},{3,0},{4,5},{5,6},{6,7},{7,4}} | collective-permute-start | bytes 56623112 | tf_op jit(solution)/shard_map/while/body/eval_jaxpr/ppermute | solution.py:83
  1709.4 560.5 %collective-permute-start.1 = (bf16[12,384,16,128]{3,1,2,0:T(8,128)(2,1)}, bf16[12,384,16,128]{3,1,2,0:T(8,128)(2,1)}, u32[]{:S(2)}, u32[]{:S(2)}) collective-permute-start(bf16[12,384,16,128]{3,1,2,0:T(8,128)(2,1)} %get-tuple-element.351), channel_id=1, source_target_pairs={{0,1},{1,2},{2,3},{3,0},{4,5},{5,6},{6,7},{7,4}} | collective-permute-start | bytes 56623112 | tf_op jit(solution)/shard_map/while/body/eval_jaxpr/ppermute | solution.py:84
  2581.3 12.6 copy-start.3
where the time goes:
time: 2600 us; the launch traced here: 2590 us
  waiting for transfers between devices  1210 us (47%)
  local copies, waits for them, and re-layouts  373 us (14%)
  starting transfers between devices  327 us (13%)
  matrix products  290 us (11%)
  other arithmetic  218 us (8%)
  blocking collectives  178 us (7%)
    ppermute x3, waiting for transfers between devices, step(): v_blk = lax.ppermute(v_blk, 'cp', shift_pairs)  607 us
    ppermute x3, waiting for transfers between devices, step(): k_blk = lax.ppermute(k_blk, 'cp', shift_pairs)  601 us
    pmax x1, blocking collectives, device_body(): head_max = lax.pmax(head_max, ('dp', 'cp'))  178 us
    ppermute x3, starting transfers between devices, step(): v_blk = lax.ppermute(v_blk, 'cp', shift_pairs)  166 us
    ppermute x3, starting transfers between devices, step(): k_blk = lax.ppermute(k_blk, 'cp', shift_pairs)  161 us
    while x6, local copies, waits for them, and re-layouts  113 us
    another operation x1, other arithmetic  107 us
    slice x2, local copies, waits for them, and re-layouts, rope_rotate(): lead_half = tensor[..., :half_dim]  103 us
  transfers between devices with their start and end apart: 6, of which 6 were waited for; matrix products, arithmetic and copies ran while one was open for 0% of the time, Pallas kernels for 0%

commit v1 on v0

v1 whole, which is shorter than its diff:
```python
import functools

import jax
import jax.numpy as jnp
from jax import lax
from jax.experimental import pallas as pl
from jax.experimental.pallas import tpu as pltpu
from jax.sharding import PartitionSpec as P


HEAD_DIM = 128
TAU_CLIP = 100.0
ROPE_THETA = 50000.0
LOG2_E = 1.4426950408889634
VMEM_LIMIT = 60 * 1024 * 1024
COL_BLOCK = 512
PROJ_BLOCK = 256
QUERY_BLOCK = 256
STEP_HEADS = 2


def rope_tables(pos_ids):
    half_dim = HEAD_DIM // 2
    lane = jnp.arange(HEAD_DIM, dtype=jnp.int32)
    freq_at = (lane % half_dim).astype(jnp.float32)
    inv_freq = jnp.float32(ROPE_THETA) ** (-freq_at * (2.0 / HEAD_DIM))
    angle = pos_ids.astype(jnp.float32)[:, None] * inv_freq[None, :]
    sin_t = jnp.sin(angle)
    return jnp.cos(angle), jnp.where(lane[None, :] < half_dim, -sin_t, sin_t)


def rotate(prod, cos_t, sin_t):
    heads = []
    for lo in range(0, prod.shape[1], HEAD_DIM):
        part = prod[:, lo:lo + HEAD_DIM]
        heads.append((part * cos_t + pltpu.roll(part, HEAD_DIM // 2, 1) * sin_t).astype(jnp.bfloat16))
    return jnp.concatenate(heads, axis=1)


def project_kernel(n_copy, lead_ref, tokens_ref, wq_ref, wk_ref, wv_ref, cos_ref, sin_ref, *refs):
    sources, (q_ref, k_ref, v_ref), copies = refs[:n_copy], refs[n_copy:n_copy + 3], refs[n_copy + 3:]
    for source, copy in zip(sources, copies):
        copy[...] = source[...]
    for row in range(q_ref.shape[0]):
        for w_ref, out_ref in ((wq_ref, q_ref), (wk_ref, k_ref), (wv_ref, v_ref)):
            prod = jnp.dot(tokens_ref[row], w_ref[...], preferred_element_type=jnp.float32)
            out_ref[row] = prod.astype(jnp.bfloat16) if w_ref is wv_ref else rotate(prod, cos_ref[...], sin_ref[...])


def project(lead, n_copy, n_rows, tokens, w_q, w_k, w_v, cos_t, sin_t):
    _, piece, d_model = tokens.shape
    width = w_q.shape[1]
    n_steps = width // PROJ_BLOCK
    w_spec = pl.BlockSpec((d_model, PROJ_BLOCK), lambda n, lead: (0, n))
    table_spec = pl.BlockSpec((piece, HEAD_DIM), lambda n, lead: (0, 0))
    out_spec = pl.BlockSpec((n_rows, piece, PROJ_BLOCK), lambda n, lead: (0, 0, n))
    out = jax.ShapeDtypeStruct((n_rows, piece, width), jnp.bfloat16)
    strip = (1, piece // n_steps, d_model)

    def source_spec(at):
        return pl.BlockSpec(strip, lambda n, lead: (lead[at], n, 0))

    return pl.pallas_call(
        functools.partial(project_kernel, n_copy),
        grid_spec=pltpu.PrefetchScalarGridSpec(
            num_scalar_prefetch=1,
            grid=(n_steps,),
            in_specs=[pl.BlockSpec((n_rows, piece, d_model), lambda n, lead: (lead[0], 0, 0)),
                      w_spec, w_spec, w_spec, table_spec, table_spec] + [source_spec(1 + i) for i in range(n_copy)],
            out_specs=[out_spec] * 3 + [pl.BlockSpec(strip, lambda n, lead: (0, n, 0))] * n_copy,
        ),
        out_shape=[out] * 3 + [jax.ShapeDtypeStruct((1, piece, d_model), jnp.bfloat16)] * n_copy,
        compiler_params=pltpu.CompilerParams(vmem_limit_bytes=VMEM_LIMIT),
        cost_estimate=pl.CostEstimate(flops=3 * 2 * n_rows * piece * d_model * width,
                                      bytes_accessed=6 * d_model * width + 8 * n_rows * piece * width,
                                      transcendentals=0),
    )(lead, tokens, w_q, w_k, w_v, cos_t, sin_t, *[tokens] * n_copy)


def row_kernel(n_proj, n_groups, index_ref, *refs):
    tokens, weights, (cos_ref, sin_ref) = refs[0:2], refs[2:5], refs[5:7]
    own, near, wo_ref = refs[7:10], refs[10:13], refs[13]
    out_refs, max_ref = refs[14:18], refs[18]
    far, qkv_scr, attn_scr = refs[-7:-4], refs[-4:-1], refs[-1]
    step = pl.program_id(0)
    piece = own[0].shape[-2]
    seq_n = 4 * piece
    starts = [pl.multiple_of(index_ref[x] * piece, piece) for x in range(4)]

    @pl.when(step < n_proj)
    def _():
        cols = pl.ds(pl.multiple_of(step * PROJ_BLOCK, PROJ_BLOCK), PROJ_BLOCK)
        for which in range(2):
            for kind in range(3):
                prod = jnp.dot(tokens[which][0], weights[kind][...], preferred_element_type=jnp.float32)
                far[kind][which, :, cols] = prod.astype(jnp.bfloat16) if kind == 2 else rotate(prod, cos_ref[which], sin_ref[which])

    @pl.when((step >= n_proj) & (step < n_proj + n_groups))
    def _():
        group = STEP_HEADS * HEAD_DIM
        group_cols = pl.ds(pl.multiple_of((step - n_proj) * group, group), group)
        for kind, scr in enumerate(qkv_scr):
            blocks = (own[kind][0], near[kind][0], far[kind][0, :, group_cols], far[kind][1, :, group_cols])
            for start, block in zip(starts, blocks):
                scr[pl.ds(start, piece), :] = block
        q_scr, k_scr, v_scr = qkv_scr
        diagonal = (lax.broadcasted_iota(jnp.int32, (QUERY_BLOCK, QUERY_BLOCK), 0)
                    >= lax.broadcasted_iota(jnp.int32, (QUERY_BLOCK, QUERY_BLOCK), 1))

        def logits(head, blk):
            lo, hi = blk * QUERY_BLOCK, (blk + 1) * QUERY_BLOCK
            cols = slice(head * HEAD_DIM, (head + 1) * HEAD_DIM)
            q_blk = q_scr[lo:hi, cols]
            dims = (((1,), (1,)), ((), ()))
            diag = lax.dot_general(q_blk, k_scr[lo:hi, cols], dims, preferred_element_type=jnp.float32)
            parts = [jnp.where(diagonal, diag, -jnp.inf)]
            if blk:
                parts.insert(0, lax.dot_general(q_blk, k_scr[:lo, cols], dims, preferred_element_type=jnp.float32))
            return parts

        items = [(head, blk) for head in range(STEP_HEADS) for blk in range(seq_n // QUERY_BLOCK)]
        tops = [jnp.full((1, 1), -jnp.inf, jnp.float32) for _ in range(STEP_HEADS)]
        ahead = logits(*items[0])
        for at, (head, blk) in enumerate(items):
            parts = ahead
            if at + 1 < len(items):
                ahead = logits(*items[at + 1])
            lo, hi = blk * QUERY_BLOCK, (blk + 1) * QUERY_BLOCK
            cols = slice(head * HEAD_DIM, (head + 1) * HEAD_DIM)
            row_max = functools.reduce(jnp.maximum, [jnp.max(s, axis=1, keepdims=True) for s in parts])
            probs = [jnp.exp2((s - row_max) * (HEAD_DIM ** -0.5 * LOG2_E)) for s in parts]
            row_sum = functools.reduce(jnp.add, [jnp.sum(p, axis=1, keepdims=True) for p in probs])
            spans = [(lo, hi)] if blk == 0 else [(0, lo), (lo, hi)]
            acc = functools.reduce(jnp.add, [
                jnp.dot(p.astype(jnp.bfloat16), v_scr[a:b, cols], preferred_element_type=jnp.float32)
                for p, (a, b) in zip(probs, spans)])
            out = (acc / row_sum).astype(jnp.bfloat16)
            out_cols = pl.ds(pl.multiple_of((step - n_proj) * group + head * HEAD_DIM, HEAD_DIM), HEAD_DIM)
            attn_scr[lo:hi, out_cols] = out
            tops[head] = jnp.maximum(tops[head], jnp.max(row_max, axis=0, keepdims=True))
        for head in range(STEP_HEADS):
            max_ref[head] = jnp.broadcast_to(tops[head] * (HEAD_DIM ** -0.5), max_ref.shape[1:])

    @pl.when(step >= n_proj + n_groups)
    def _():
        for start, o_ref in zip(starts, out_refs):
            o_ref[...] = jnp.dot(attn_scr[pl.ds(start, piece), :], wo_ref[...],
                                 preferred_element_type=jnp.float32).astype(jnp.bfloat16)


def row_block(index, tokens, weights, cos_t, sin_t, own, near, w_o, spare=None):
    _, piece, width = own[0].shape
    n_heads = width // HEAD_DIM
    d_model = w_o.shape[1]
    seq_n = 4 * piece
    n_proj, n_out = width // PROJ_BLOCK, d_model // COL_BLOCK
    n_groups, group = n_heads // STEP_HEADS, STEP_HEADS * HEAD_DIM

    def group_at(s):
        return jnp.clip(s - n_proj, 0, n_groups - 1)

    def out_at(s):
        return jnp.maximum(s - n_proj - n_groups, 0)

    token_spec = pl.BlockSpec((1, piece, d_model), lambda s, ix: (0, 0, 0))
    w_spec = pl.BlockSpec((d_model, PROJ_BLOCK), lambda s, ix: (0, jnp.minimum(s, n_proj - 1)))
    table_spec = pl.BlockSpec((2, piece, HEAD_DIM), lambda s, ix: (0, 0, 0))
    near_spec = pl.BlockSpec((1, piece, group), lambda s, ix: (ix[4], 0, group_at(s)))
    out_spec = pl.BlockSpec((piece, COL_BLOCK), lambda s, ix: (0, out_at(s)))
    out = jax.ShapeDtypeStruct((piece, d_model), jnp.bfloat16)
    extra = [] if spare is None else [jax.ShapeDtypeStruct(spare, jnp.bfloat16)]
    return pl.pallas_call(
        functools.partial(row_kernel, n_proj, n_groups),
        grid_spec=pltpu.PrefetchScalarGridSpec(
            num_scalar_prefetch=1,
            grid=(n_proj + n_groups + n_out,),
            in_specs=[token_spec] * 2 + [w_spec] * 3 + [table_spec] * 2 + [near_spec] * 6
            + [pl.BlockSpec((width, COL_BLOCK), lambda s, ix: (0, out_at(s)))],
            out_specs=[out_spec] * 4 + [pl.BlockSpec((STEP_HEADS, 8, 128), lambda s, ix: (group_at(s), 0, 0))]
            + [pl.BlockSpec(memory_space=pltpu.HBM)] * len(extra),
            scratch_shapes=[pltpu.VMEM((2, piece, width), jnp.bfloat16)] * 3
            + [pltpu.VMEM((seq_n, group), jnp.bfloat16)] * 3 + [pltpu.VMEM((seq_n, width), jnp.bfloat16)],
        ),
        out_shape=[out] * 4 + [jax.ShapeDtypeStruct((n_heads, 8, 128), jnp.float32)] + extra,
        compiler_params=pltpu.CompilerParams(vmem_limit_bytes=VMEM_LIMIT),
        cost_estimate=pl.CostEstimate(flops=5 * seq_n * width * d_model + 4 * seq_n * seq_n * width,
                                      bytes_accessed=8 * width * d_model + 8 * seq_n * width,
                                      transcendentals=seq_n * seq_n * n_heads // 2),
    )(index, *tokens, *weights, cos_t, sin_t, *own, *near, w_o)


def place_kernel(n_chunks, rows_ref, whole_ref, *refs):
    step = pl.program_id(0)
    for at, chunk_ref in enumerate(refs[:n_chunks]):
        @pl.when(step // 2 == at)
        def _():
            @pl.loop(0, chunk_ref.shape[0] // 32)
            def _(part):
                rows = pl.ds(pl.multiple_of(part * 32, 32), 32)
                refs[-1][0, rows, :] = chunk_ref[rows, :]


def place(whole, chunks, rows):
    piece, d_model = chunks[0].shape
    strip = piece // 2

    def chunk_spec(at):
        return pl.BlockSpec((strip, d_model), lambda i, rows: (jnp.clip(i - 2 * at, 0, 1), 0))

    return pl.pallas_call(
        functools.partial(place_kernel, len(chunks)),
        grid_spec=pltpu.PrefetchScalarGridSpec(
            num_scalar_prefetch=1,
            grid=(2 * len(chunks),),
            in_specs=[pl.BlockSpec(memory_space=pltpu.HBM)] + [chunk_spec(at) for at in range(len(chunks))],
            out_specs=pl.BlockSpec((1, strip, d_model), lambda i, rows: (rows[i // 2], i % 2, 0)),
        ),
        out_shape=jax.ShapeDtypeStruct(whole.shape, whole.dtype),
        input_output_aliases={1: 0},
        cost_estimate=pl.CostEstimate(flops=len(chunks) * piece * d_model, bytes_accessed=4 * len(chunks) * piece * d_model,
                                      transcendentals=0),
    )(jnp.stack(rows), whole, *chunks)


def clip_weights(head_max, w_q, w_k):
    factor = jnp.where(head_max > TAU_CLIP, jnp.sqrt(TAU_CLIP / head_max), 1.0)
    col_factor = jnp.repeat(factor, HEAD_DIM)[None, :]
    return (w_q.astype(jnp.float32) * col_factor).astype(jnp.bfloat16), (w_k.astype(jnp.float32) * col_factor).astype(jnp.bfloat16)


def solution(mesh):
    cp_size = mesh.shape["cp"]
    pairs = {x: [(i, i ^ x) for i in range(cp_size)] for x in range(1, cp_size)}

    def layer(hidden, pos_ids, w_q, w_k, w_v, w_o):
        rank = lax.axis_index("cp")
        batch_n, piece, d_model = hidden.shape
        n_rows = batch_n // cp_size
        peer = [rank ^ x for x in range(cp_size)]
        weights = (w_q, w_k, w_v)
        zero = jnp.zeros((1,), jnp.int32)

        def swap(value, x):
            return lax.ppermute(value, "cp", pairs[x])

        def slab(source, x, row, count):
            return lax.dynamic_slice(source, (peer[x] * n_rows + row, 0, 0), (count, piece, d_model))

        first = [slab(hidden, x, 0, 1) for x in (2, 3)]
        hidden_b, pos_b, _ = lax.optimization_barrier((hidden, pos_ids, first))
        near_in = swap(slab(hidden_b, 1, 0, n_rows), 1)
        pos_near, *pos_far = [swap(pos_b, x) for x in range(1, cp_size)]
        later = [(row, x) for row in range(1, n_rows) for x in (2, 3)]
        lead = jnp.stack([peer[0]] + [peer[x] * n_rows + row for row, x in later])
        *own, a, b, c, d = project(lead, len(later), n_rows, hidden, *weights, *rope_tables(pos_ids))
        far_slabs = [first, [a, b], [c, d]]
        far = [[swap(value, x) for value, x in zip(slabs, (2, 3))] for slabs in far_slabs]

        near_in, pos_near, _ = lax.optimization_barrier((near_in, pos_near, own[0]))
        near = project(zero, 0, n_rows, near_in, *weights, *rope_tables(pos_near))

        pos_far, _ = lax.optimization_barrier((pos_far, near[0]))
        far_tables = [t.reshape(2, piece, HEAD_DIM) for t in rope_tables(jnp.concatenate(pos_far))]
        outs, maxes = [], []
        before = near[0]
        for row in range(n_rows):
            last = row == n_rows - 1
            tokens, _ = lax.optimization_barrier((far[row], before))
            got = row_block(jnp.stack([*peer, jnp.int32(row)]), tokens, weights, *far_tables, own, near, w_o, hidden.shape if last else None)
            before = got[4]
            maxes.append(got[4][:, 0, 0])
            outs.append([got[0]] + [swap(got[x], x) for x in range(1, cp_size)])
        out = got[5]
        top = functools.reduce(jnp.maximum, maxes)
        top = jnp.maximum(top, lax.ppermute(top, "dp", [(0, 1), (1, 0)]))
        top = jnp.maximum(top, swap(top, 1))
        head_max = jnp.maximum(top, swap(top, 2))
        out, _ = lax.optimization_barrier((out, top))
        early = [(row, x) for row in range(n_rows - 1) for x in range(cp_size)]
        out = place(out, [outs[row][x] for row, x in early], [peer[x] * n_rows + row for row, x in early])
        for x in range(cp_size):
            out = lax.dynamic_update_slice(out, outs[-1][x][None], (peer[x] * n_rows + n_rows - 1, 0, 0))
        w_q_new, w_k_new = clip_weights(head_max, w_q, w_k)
        return out, head_max, w_q_new, w_k_new

    return jax.shard_map(
        layer,
        mesh=mesh,
        in_specs=(P("dp", "cp", None), P("cp"), P(None, None), P(None, None), P(None, None), P(None, None)),
        out_specs=(P("dp", "cp", None), P(None), P(None, None), P(None, None)),
        check_vma=False,
    )
```

time: 2600 us -> 533 us (0.20)
  waiting for transfers between devices: 1210 us -> 145 us
  local copies, waits for them, and re-layouts: 373 us -> 20.1 us
  Pallas kernels: 0 us -> 327 us
  starting transfers between devices: 327 us -> 18.5 us
  matrix products: 290 us -> 0 us
  other arithmetic: 218 us -> 19.7 us
  blocking collectives: 178 us -> 0 us
    ppermute x6 -> x22, waiting for transfers between devices: 1210 us -> 145 us  [the longest x21 144 us: swap(): return lax.ppermute(value, 'cp', pairs[x])]
    pallas_call x0 -> x6, Pallas kernels: none -> 327 us  [the longest x3 235 us: row_block(): pl.pallas_call(functools.partial(row_kernel, n_proj, n_groups), grid_spec...]
    ppermute x6 -> x22, starting transfers between devices: 327 us -> 18.5 us  [the longest x21 17 us: swap(): return lax.ppermute(value, 'cp', pairs[x])]
    dot_general x6 -> x0, matrix products: 290 us -> none  [the longest x1 56.4 us: attend_block(): jnp.einsum('bhqk,bkhd->bqhd', prob_w.astype(jnp.bfloat16), v_blk, preferr...]
    while x8 -> x0, local copies, waits for them, and re-layouts: 186 us -> none
    pmax x1 -> x0, blocking collectives: 178 us -> none  [device_body(): head_max = lax.pmax(head_max, ('dp', 'cp'))]
    another operation x2 -> x0, other arithmetic: 108 us -> none
    slice x2 -> x0, local copies, waits for them, and re-layouts: 103 us -> none  [rope_rotate(): lead_half = tensor[..., :half_dim]]
  transfers between devices with their start and end apart: 6 -> 22, of which waited for: 6 -> 8; matrix products, arithmetic and copies ran while one was open for 0% -> 6% of each run, Pallas kernels for 0% -> 62%
where the time goes in v1:
time: 533 us; the launch traced here: 531 us
  Pallas kernels  327 us (61%)
  waiting for transfers between devices  145 us (27%)
  local copies, waits for them, and re-layouts  20.1 us (4%)
  other arithmetic  19.7 us (4%)
  starting transfers between devices  18.5 us (3%)
    pallas_call x3, Pallas kernels, row_block(): pl.pallas_call(functools.partial(row_kernel, n_proj, n_groups), grid_spec...  235 us
    ppermute x21, waiting for transfers between devices, swap(): return lax.ppermute(value, 'cp', pairs[x])  144 us
    pallas_call x2, Pallas kernels, project(): pl.pallas_call(functools.partial(project_kernel, n_copy), grid_spec=pltpu...  74.7 us
    pallas_call x1, Pallas kernels, place(): pl.pallas_call(functools.partial(place_kernel, len(chunks)), grid_spec=pl...  17.8 us
    ppermute x21, starting transfers between devices, swap(): return lax.ppermute(value, 'cp', pairs[x])  17 us
    convert_element_type x1, other arithmetic, clip_weights(): (w_k.astype(jnp.float32) * col_factor).astype(jnp.bfloat16)  12.5 us
  transfers between devices with their start and end apart: 22, of which 8 were waited for; matrix products, arithmetic and copies ran while one was open for 6% of the time, Pallas kernels for 62%

profile of v1, /device:TPU:0, one launch (start us, length us, event | category | flops | bytes accessed | tf_op | source)
XLA Modules:
  0.0 531.4 jit_solution(18313181477427742664)
XLA Ops:
  0.7 2.1 constant_dynamic-slice_fusion.1
  2.8 5.2 constant_dynamic-slice_fusion
  8.9 2.6 collective-permute-start.9
  11.6 2.0 collective-permute-start.5
  14.2 1.5 negate_select_fusion.2
  15.8 38.5 %shard_map.93 = (bf16[3,384,2048]{2,1,0:T(8,128)(2,1)}, bf16[3,384,2048]{2,1,0:T(8,128)(2,1)}, bf16[3,384,2048]{2,1,0:T(8,128)(2,1)}, bf16[1,384,2048]{2,1,0:T(8...) custom-call(s32[5]{0:T(128)} %stack.84.lead_ref, ...), custom_call_target="tpu_custom_call" | custom-call | flops 28991029248 | bytes 44040192 | tf_op jit(solution)/shard_map/pallas_call | solution.py:63
  56.1 2.0 collective-permute-start
  59.7 36.3 %shard_map.94 = (bf16[3,384,2048]{2,1,0:T(8,128)(2,1)}, bf16[3,384,2048]{2,1,0:T(8,128)(2,1)}, bf16[3,384,2048]{2,1,0:T(8,128)(2,1)}) custom-call(s32[1]{0:T(128)} %constant.58.clone.1.lead_ref, bf16[3,384,2048]{2,1,0:T(8,128)(2,1)} %collective-permute-done.6.tokens_ref, bf16[2048,2048]{1,0:T(8,128)(2,1)} %refs_2_.7, bf16[2048,2048]{1,0:T(8,128)(2,1)} %refs_3_.7, ...), custom_call_target="tpu_custom_call" | custom-call | flops 28991029248 | bytes 44040192 | tf_op jit(solution)/shard_map/pallas_call | solution.py:63
  97.8 2.5 negate_select_fusion
  100.3 78.1 %shard_map.95 = (bf16[384,2048]{1,0:T(8,128)(2,1)}, bf16[384,2048]{1,0:T(8,128)(2,1)}, bf16[384,2048]{1,0:T(8,128)(2,1)}, bf16[384,2048]{1,0:T(8,128)(2,1)}, f32[16,8,128]{2,1,0:T(8,128)}) custom-call(s32[5]{0:T(128)} %stack.86.index_ref, bf16[1,384,2048]{2,1,0:T(8,128)(2,1)} %collective-permute-done.4.refs_0_, ...), custom_call_target="tpu_custom_call" | custom-call | flops 51539607552 | bytes 58720256 | tf_op jit(solution)/shard_map/pallas_call | solution.py:172
  178.5 16.2 %collective-permute-done.2.refs_0_ = bf16[1,384,2048]{2,1,0:T(8,128)(2,1)} collective-permute-done((bf16[1,384,2048]{2,1,0:T(8,128)(2,1)}, bf16[1,384,2048]{2,1,0:T(8,128)(2,1)}, u32[]{:S(2)}, u32[]{:S(2)}) %collective-permute-start.2) | collective-permute-done | bytes 1572896 | tf_op jit(solution)/shard_map/ppermute | solution.py:244
  194.6 31.7 %collective-permute-done.3.refs_1_ = bf16[1,384,2048]{2,1,0:T(8,128)(2,1)S(1)} collective-permute-done((bf16[1,384,2048]{2,1,0:T(8,128)(2,1)}, bf16[1,384,2048]{2,1,0:T(8,128)(2,1)S(1)}, u32[]{:S(2)}, u32[]{:S(2)}) %collective-permute-start.3) | collective-permute-done | bytes 1572896 | tf_op jit(solution)/shard_map/ppermute | solution.py:244
  229.6 78.2 %shard_map.96 = (bf16[384,2048]{1,0:T(8,128)(2,1)}, bf16[384,2048]{1,0:T(8,128)(2,1)}, bf16[384,2048]{1,0:T(8,128)(2,1)}, bf16[384,2048]{1,0:T(8,128)(2,1)}, f32[16,8,128]{2,1,0:T(8,128)}) custom-call(s32[5]{0:T(128)} %stack.85.index_ref, bf16[1,384,2048]{2,1,0:T(8,128)(2,1)} %collective-permute-done.2.refs_0_, bf16[1,384,2048]{2,1,0:T(8,128)(2,1)} %copy-done.5, ...), custom_call_target="tpu_custom_call" | custom-call | flops 51539607552 | bytes 58720256 | tf_op jit(solution)/shard_map/pallas_call | solution.py:172
  307.8 78.2 %shard_map.97 = (bf16[384,2048]{1,0:T(8,128)(2,1)}, bf16[384,2048]{1,0:T(8,128)(2,1)}, bf16[384,2048]{1,0:T(8,128)(2,1)}, bf16[384,2048]{1,0:T(8,128)(2,1)}, f32...) custom-call(s32[5]{0:T(128)} %stack.81.index_ref, bf16[1,384,2048]{2,1,0:T(8,128)(2,1)} %collective-permute-done.refs_0_, ...), custom_call_target="tpu_custom_call" | custom-call | flops 51539607552 | bytes 58720256 | tf_op jit(solution)/shard_map/pallas_call | solution.py:172
  392.3 3.2 collective-permute-done.21
  396.5 1.7 collective-permute-start.16
  398.3 12.5 %multiply_convert_fusion = (bf16[2048,2048]{1,0:T(8,128)(2,1)}, bf16[2048,2048]{1,0:T(8,128)(2,1)}) fusion(bf16[2048,2048]{1,0:T(8,128)(2,1)} %refs_3_.7, f32[2048]{0:T(1024)S(1)} %broadcast_bitcast_fusion, bf16[2048,2048]{1,0:T(8,128)(2,1)} %refs_2_.7), kind=kLoop, calls=%fused_computation | loop fusion | flops 25165824 | bytes 33562624 | tf_op jit(solution)/shard_map/convert_element_type | solution.py:228
  412.0 1.6 collective-permute-start.20
  413.6 53.2 %collective-permute-done.16.refs_6_ = bf16[384,2048]{1,0:T(8,128)(2,1)} collective-permute-done((bf16[384,2048]{1,0:T(8,128)(2,1)}, bf16[384,2048]{1,0:T(8,128)(2,1)}, u32[]{:S(2)}, u32[]{:S(2)}) %collective-permute-start.16) | collective-permute-done | bytes 1572896 | tf_op jit(solution)/shard_map/ppermute | solution.py:244
  466.7 31.6 %collective-permute-done.17.refs_7_ = bf16[384,2048]{1,0:T(8,128)(2,1)} collective-permute-done((bf16[384,2048]{1,0:T(8,128)(2,1)}, bf16[384,2048]{1,0:T(8,128)(2,1)}, u32[]{:S(2)}, u32[]{:S(2)}) %collective-permute-start.17) | collective-permute-done | bytes 1572896 | tf_op jit(solution)/shard_map/ppermute | solution.py:244
  498.4 17.8 %shard_map.98 = bf16[12,384,2048]{2,1,0:T(8,128)(2,1)} custom-call(s32[8]{0:T(128)} %stack.76.rows_ref, bf16[12,384,2048]{2,1,0:T(8,128)(2,1)} %get-tuple-element.69.whole_ref, bf16[384,2048]{1,0:T(8,128)(2,1)} %get-tuple-element.70.refs_0_, bf16[384,2048]{1,0:T(8,128)(2,1)} %copy-done, bf16[384,2048]{1,0:T(8,128)(2,1)} %copy-done.1, ...), custom_call_target="tpu_custom_call", output_to_operand_aliasing={{}: (1, {})} | custom-call | flops 6291456 | bytes 25165824 | tf_op jit(solution)/shard_map/pallas_call | solution.py:210
  517.4 2.7 bitcast_dynamic-update-slice_fusion.2
  520.1 2.7 bitcast_dynamic-update-slice_fusion.1
  522.9 7.3 %collective-permute-done.20 = bf16[384,2048]{1,0:T(8,128)(2,1)S(1)} collective-permute-done((bf16[384,2048]{1,0:T(8,128)(2,1)}, bf16[384,2048]{1,0:T(8,128)(2,1)S(1)}, u32[]{:S(2)}, u32[]{:S(2)}) %collective-permute-start.20) | collective-permute-done | bytes 1572896 | tf_op jit(solution)/shard_map/ppermute | solution.py:244
  (66 shorter events, 21.2 us)
Async XLA Ops:
  8.0 48.1 %collective-permute-start.6 = (bf16[3,384,2048]{2,1,0:T(8,128)(2,1)}, bf16[3,384,2048]{2,1,0:T(8,128)(2,1)}, u32[]{:S(2)}, u32[]{:S(2)}) collective-permute-start(bf16[3,384,2048]{2,1,0:T(8,128)(2,1)} %constant_dynamic-slice_fusion), channel_id=1, source_target_pairs={{0,1},{1,0},{2,3},{3,2},{4,5},{5,4},{6,7},{7,6}} | collective-permute-start | bytes 14155784 | tf_op jit(solution)/shard_map/ppermute | solution.py:244
  8.9 87.1 %collective-permute-start.9 = (s32[384]{0:T(512)S(1)}, s32[384]{0:T(512)S(1)}, u32[]{:S(2)}, u32[]{:S(2)}) collective-permute-start(s32[384]{0:T(512)S(1)} %copy-done.4), channel_id=1, source_target_pairs={{0,3},{1,2},{2,1},{3,0},{4,7},{5,6},{6,5},{7,4}} | collective-permute-start | bytes 4616 | tf_op jit(solution)/shard_map/ppermute | solution.py:244
  11.5 84.5 %collective-permute-start.8 = (s32[384]{0:T(512)S(1)}, s32[384]{0:T(512)S(1)}, u32[]{:S(2)}, u32[]{:S(2)}) collective-permute-start(s32[384]{0:T(512)S(1)} %copy-done.4), channel_id=1, source_target_pairs={{0,2},{1,3},{2,0},{3,1},{4,6},{5,7},{6,4},{7,5}} | collective-permute-start | bytes 4616 | tf_op jit(solution)/shard_map/ppermute | solution.py:244
  11.5 44.7 %collective-permute-start.7 = (s32[384]{0:T(512)S(1)}, s32[384]{0:T(512)S(1)}, u32[]{:S(2)}, u32[]{:S(2)}) collective-permute-start(s32[384]{0:T(512)S(1)} %copy-done.4), channel_id=1, source_target_pairs={{0,1},{1,0},{2,3},{3,2},{4,5},{5,4},{6,7},{7,6}} | collective-permute-start | bytes 4616 | tf_op jit(solution)/shard_map/ppermute | solution.py:244
  11.6 85.5 %collective-permute-start.5 = (bf16[1,384,2048]{2,1,0:T(8,128)(2,1)S(1)}, bf16[1,384,2048]{2,1,0:T(8,128)(2,1)}, u32[]{:S(2)}, u32[]{:S(2)}) collective-permute-start(bf16[1,384,2048]{2,1,0:T(8,128)(2,1)S(1)} %get-tuple-element.84), channel_id=1, source_target_pairs={{0,3},{1,2},{2,1},{3,0},{4,7},{5,6},{6,5},{7,4}} | collective-permute-start | bytes 4718600 | tf_op jit(solution)/shard_map/ppermute | solution.py:244
  56.1 41.6 %collective-permute-start.4 = (bf16[1,384,2048]{2,1,0:T(8,128)(2,1)S(1)}, bf16[1,384,2048]{2,1,0:T(8,128)(2,1)}, u32[]{:S(2)}, u32[]{:S(2)}) collective-permute-start(bf16[1,384,2048]{2,1,0:T(8,128)(2,1)S(1)} %get-tuple-element.85), channel_id=1, source_target_pairs={{0,2},{1,3},{2,0},{3,1},{4,6},{5,7},{6,4},{7,5}} | collective-permute-start | bytes 4718600 | tf_op jit(solution)/shard_map/ppermute | solution.py:244
  56.1 251.6 %collective-permute-start = (bf16[1,384,2048]{2,1,0:T(8,128)(2,1)}, bf16[1,384,2048]{2,1,0:T(8,128)(2,1)}, u32[]{:S(2)}, u32[]{:S(2)}) collective-permute-start(bf16[1,384,2048]{2,1,0:T(8,128)(2,1)} %get-tuple-element.43), channel_id=1, source_target_pairs={{0,2},{1,3},{2,0},{3,1},{4,6},{5,7},{6,4},{7,5}} | collective-permute-start | bytes 4718600 | tf_op jit(solution)/shard_map/ppermute | solution.py:244
  95.9 211.8 %collective-permute-start.1 = (bf16[1,384,2048]{2,1,0:T(8,128)(2,1)}, bf16[1,384,2048]{2,1,0:T(8,128)(2,1)}, u32[]{:S(2)}, u32[]{:S(2)}) collective-permute-start(bf16[1,384,2048]{2,1,0:T(8,128)(2,1)} %get-tuple-element.44), channel_id=1, source_target_pairs={{0,3},{1,2},{2,1},{3,0},{4,7},{5,6},{6,5},{7,4}} | collective-permute-start | bytes 4718600 | tf_op jit(solution)/shard_map/ppermute | solution.py:244
  96.0 98.6 %collective-permute-start.2 = (bf16[1,384,2048]{2,1,0:T(8,128)(2,1)}, bf16[1,384,2048]{2,1,0:T(8,128)(2,1)}, u32[]{:S(2)}, u32[]{:S(2)}) collective-permute-start(bf16[1,384,2048]{2,1,0:T(8,128)(2,1)} %get-tuple-element.45), channel_id=1, source_target_pairs={{0,2},{1,3},{2,0},{3,1},{4,6},{5,7},{6,4},{7,5}} | collective-permute-start | bytes 4718600 | tf_op jit(solution)/shard_map/ppermute | solution.py:244
  97.0 129.2 %collective-permute-start.3 = (bf16[1,384,2048]{2,1,0:T(8,128)(2,1)}, bf16[1,384,2048]{2,1,0:T(8,128)(2,1)S(1)}, u32[]{:S(2)}, u32[]{:S(2)}) collective-permute-start(bf16[1,384,2048]{2,1,0:T(8,128)(2,1)} %get-tuple-element.46), channel_id=1, source_target_pairs={{0,3},{1,2},{2,1},{3,0},{4,7},{5,6},{6,5},{7,4}} | collective-permute-start | bytes 4718600 | tf_op jit(solution)/shard_map/ppermute | solution.py:244
  226.3 170.1 %collective-permute-start.12 = (bf16[384,2048]{1,0:T(8,128)(2,1)}, bf16[384,2048]{1,0:T(8,128)(2,1)S(1)}, u32[]{:S(2)}, u32[]{:S(2)}) collective-permute-start(bf16[384,2048]{1,0:T(8,128)(2,1)} %get-tuple-element.71), channel_id=1, source_target_pairs={{0,1},{1,0},{2,3},{3,2},{4,5},{5,4},{6,7},{7,6}} | collective-permute-start | bytes 4718600 | tf_op jit(solution)/shard_map/ppermute | solution.py:244
  227.4 169.0 %collective-permute-start.13 = (bf16[384,2048]{1,0:T(8,128)(2,1)}, bf16[384,2048]{1,0:T(8,128)(2,1)S(1)}, u32[]{:S(2)}, u32[]{:S(2)}) collective-permute-start(bf16[384,2048]{1,0:T(8,128)(2,1)} %get-tuple-element.72), channel_id=1, source_target_pairs={{0,2},{1,3},{2,0},{3,1},{4,6},{5,7},{6,4},{7,5}} | collective-permute-start | bytes 4718600 | tf_op jit(solution)/shard_map/ppermute | solution.py:244
  228.2 169.9 %collective-permute-start.14 = (bf16[384,2048]{1,0:T(8,128)(2,1)}, bf16[384,2048]{1,0:T(8,128)(2,1)}, u32[]{:S(2)}, u32[]{:S(2)}) collective-permute-start(bf16[384,2048]{1,0:T(8,128)(2,1)} %get-tuple-element.73), channel_id=1, source_target_pairs={{0,3},{1,2},{2,1},{3,0},{4,7},{5,6},{6,5},{7,4}} | collective-permute-start | bytes 4718600 | tf_op jit(solution)/shard_map/ppermute | solution.py:244
  387.1 3.6 collective-permute-start.10
  390.7 1.2 collective-permute-start.11
  390.7 126.7 %collective-permute-start.18 = (bf16[384,2048]{1,0:T(8,128)(2,1)}, bf16[384,2048]{1,0:T(8,128)(2,1)}, u32[]{:S(2)}, u32[]{:S(2)}) collective-permute-start(bf16[384,2048]{1,0:T(8,128)(2,1)} %get-tuple-element.79), channel_id=1, source_target_pairs={{0,1},{1,0},{2,3},{3,2},{4,5},{5,4},{6,7},{7,6}} | collective-permute-start | bytes 4718600 | tf_op jit(solution)/shard_map/ppermute | solution.py:244
  391.9 3.6 collective-permute-start.21
  395.4 124.7 %collective-permute-start.19 = (bf16[384,2048]{1,0:T(8,128)(2,1)}, bf16[384,2048]{1,0:T(8,128)(2,1)}, u32[]{:S(2)}, u32[]{:S(2)}) collective-permute-start(bf16[384,2048]{1,0:T(8,128)(2,1)} %get-tuple-element.80), channel_id=1, source_target_pairs={{0,2},{1,3},{2,0},{3,1},{4,6},{5,7},{6,4},{7,5}} | collective-permute-start | bytes 4718600 | tf_op jit(solution)/shard_map/ppermute | solution.py:244
  396.4 14.3 %copy-start = (bf16[384,2048]{1,0:T(8,128)(2,1)}, bf16[384,2048]{1,0:T(8,128)(2,1)S(1)}, u32[]{:S(2)}) copy-start(bf16[384,2048]{1,0:T(8,128)(2,1)S(1)} %collective-permute-done.12.refs_1_) | copy-start | bytes 4718596
  396.4 14.3 %collective-permute-start.15 = (bf16[384,2048]{1,0:T(8,128)(2,1)}, bf16[384,2048]{1,0:T(8,128)(2,1)S(1)}, u32[]{:S(2)}, u32[]{:S(2)}) collective-permute-start(bf16[384,2048]{1,0:T(8,128)(2,1)} %get-tuple-element.75), channel_id=1, source_target_pairs={{0,1},{1,0},{2,3},{3,2},{4,5},{5,4},{6,7},{7,6}} | collective-permute-start | bytes 4718600 | tf_op jit(solution)/shard_map/ppermute | solution.py:244
  396.5 70.3 %collective-permute-start.16 = (bf16[384,2048]{1,0:T(8,128)(2,1)}, bf16[384,2048]{1,0:T(8,128)(2,1)}, u32[]{:S(2)}, u32[]{:S(2)}) collective-permute-start(bf16[384,2048]{1,0:T(8,128)(2,1)} %get-tuple-element.76), channel_id=1, source_target_pairs={{0,2},{1,3},{2,0},{3,1},{4,6},{5,7},{6,4},{7,5}} | collective-permute-start | bytes 4718600 | tf_op jit(solution)/shard_map/ppermute | solution.py:244
  398.1 100.2 %collective-permute-start.17 = (bf16[384,2048]{1,0:T(8,128)(2,1)}, bf16[384,2048]{1,0:T(8,128)(2,1)}, u32[]{:S(2)}, u32[]{:S(2)}) collective-permute-start(bf16[384,2048]{1,0:T(8,128)(2,1)} %get-tuple-element.77), channel_id=1, source_target_pairs={{0,3},{1,2},{2,1},{3,0},{4,7},{5,6},{6,5},{7,4}} | collective-permute-start | bytes 4718600 | tf_op jit(solution)/shard_map/ppermute | solution.py:244
  412.0 118.1 %collective-permute-start.20 = (bf16[384,2048]{1,0:T(8,128)(2,1)}, bf16[384,2048]{1,0:T(8,128)(2,1)S(1)}, u32[]{:S(2)}, u32[]{:S(2)}) collective-permute-start(bf16[384,2048]{1,0:T(8,128)(2,1)} %get-tuple-element.81), channel_id=1, source_target_pairs={{0,3},{1,2},{2,1},{3,0},{4,7},{5,6},{6,5},{7,4}} | collective-permute-start | bytes 4718600 | tf_op jit(solution)/shard_map/ppermute | solution.py:244
  498.4 17.8 %copy-start.3 = (bf16[384,2048]{1,0:T(8,128)(2,1)S(1)}, bf16[384,2048]{1,0:T(8,128)(2,1)}, u32[]{:S(2)}) copy-start(bf16[384,2048]{1,0:T(8,128)(2,1)} %get-tuple-element.78) | copy-start | bytes 4718596
  (4 other events, 22.8 us)
